TPU v7x, 32 devices: a whole 2x2x4 slice. The times are simulated.
32 devices in a mesh: row: 8 (over z, x), col: 4 (over y, core).
Axes of the slice: x: 2, y: 2, z: 4, core: 2. Of those that a mesh axis runs over, the one named last changes fastest.
Arguments:
- visible_data: bfloat16 [512, 32768], P('col', 'row'), may hold values from 0 to 1
- hidden_uniform: float32 [512, 16384], P('row', 'col'), may hold values from 0.01 to 0.99
- visible_uniform: float32 [512, 32768], P('col', 'row'), may hold values from 0.01 to 0.99
- weights: bfloat16 [32768, 16384], P('row', 'col'), may hold values from -0.03125 to 0.03125
- visible_bias: float32 [32768], P('row'), may hold values from -4 to 4
- hidden_bias: float32 [16384], P('col'), may hold values from -4 to 4
Outputs:
- grad_weights: bfloat16 [32768, 16384], P('row', 'col')
- grad_visible: float32 [32768], P('row')
- grad_hidden: float32 [16384], P('col')
- hidden_sample: bfloat16 [512, 16384], P('row', 'col')
- reconstruction: bfloat16 [512, 32768], P('col', 'row')
All inputs are finite; a program needn't handle non-finite values.
Results may differ from a plain program's by a relative error of at most 0.0034.
Values may be sent and summed in bfloat16 or wider, within the bound.
A program may use at most 192 MiB of HBM per device.

v0:
```python
import jax
import jax.numpy as jnp
from jax import lax
from jax.sharding import PartitionSpec as P


def relaxed(field, uniform):
    return jax.nn.sigmoid(2.0 * (field + jnp.log(uniform) - jnp.log1p(-uniform)))


def on_device(visible_data, hidden_uniform, visible_uniform, weights, visible_bias, hidden_bias):
    row_count = lax.axis_size("row")
    col_count = lax.axis_size("col")
    batch_total = visible_data.shape[0] * col_count
    hidden_rows_dev = batch_total // row_count
    visible_rows_dev = batch_total // col_count
    transposed = (((1,), (1,)), ((), ()))
    visible_full = lax.all_gather(visible_data, "col", axis=0, tiled=True)

    def hidden_field(source):
        partial_value = jnp.dot(source, weights, preferred_element_type=jnp.float32)
        narrow = hidden_bias.shape[0] // row_count
        own_bias = lax.dynamic_slice_in_dim(hidden_bias, lax.axis_index("row") * narrow, narrow, 0)
        return lax.psum_scatter(partial_value, "row", scatter_dimension=1, tiled=True) + own_bias

    field_pos = hidden_field(visible_full)
    probs_pos = jax.nn.sigmoid(field_pos).astype(jnp.bfloat16)
    hidden_numbers = lax.all_to_all(hidden_uniform, "row", split_axis=1, concat_axis=0, tiled=True)
    sample_pos = relaxed(field_pos, hidden_numbers).astype(jnp.bfloat16)
    sample_full, probs_full = (
        lax.all_gather(sample_pos, "row", axis=1, tiled=True),
        lax.all_gather(probs_pos, "row", axis=1, tiled=True),
    )
    visible_partial = lax.dot_general(
        sample_full, weights, transposed, preferred_element_type=jnp.float32
    )
    narrow_vis = visible_bias.shape[0] // col_count
    own_visible_bias = lax.dynamic_slice_in_dim(
        visible_bias, lax.axis_index("col") * narrow_vis, narrow_vis, 0
    )
    field_neg = (
        lax.psum_scatter(visible_partial, "col", scatter_dimension=1, tiled=True) + own_visible_bias
    )
    visible_numbers = lax.all_to_all(
        visible_uniform, "col", split_axis=1, concat_axis=0, tiled=True
    )
    recon_own = relaxed(field_neg, visible_numbers).astype(jnp.bfloat16)
    recon_full = lax.all_gather(recon_own, "col", axis=1, tiled=True)
    probs_back = jax.nn.sigmoid(hidden_field(recon_full)).astype(jnp.bfloat16)
    negative_full = lax.all_gather(probs_back, "row", axis=1, tiled=True)
    contract_batch = (((0,), (0,)), ((), ()))
    left_side = jnp.concatenate([visible_full, recon_full], axis=0)
    right_side = jnp.concatenate([probs_full, -negative_full], axis=0)
    difference = lax.dot_general(
        left_side, right_side, contract_batch, preferred_element_type=jnp.float32
    )
    grad_weights = (difference / batch_total).astype(jnp.bfloat16)
    grad_visible = jnp.mean(
        visible_full.astype(jnp.float32) - recon_full.astype(jnp.float32), axis=0
    )
    grad_hidden = jnp.mean(
        probs_full.astype(jnp.float32) - negative_full.astype(jnp.float32), axis=0
    )
    hidden_sample = lax.dynamic_slice_in_dim(
        sample_full, lax.axis_index("row") * hidden_rows_dev, hidden_rows_dev, 0
    )
    reconstruction = lax.dynamic_slice_in_dim(
        recon_full, lax.axis_index("col") * visible_rows_dev, visible_rows_dev, 0
    )
    return (grad_weights, grad_visible, grad_hidden, hidden_sample, reconstruction)


def solution(mesh):
    placed = (
        P("col", "row"),
        P("row", "col"),
        P("col", "row"),
        P("row", "col"),
        P("row"),
        P("col"),
    )
    return jax.shard_map(
        on_device,
        mesh=mesh,
        in_specs=placed,
        out_specs=(P("row", "col"), P("row"), P("col"), P("row", "col"), P("col", "row")),
        check_vma=False,
    )
```

profile of v0, /device:TPU:0, one launch (start us, length us, event | category | flops | bytes accessed | tf_op | source)
XLA Modules:
  0.0 841.3 jit_solution(14518315988730816402)
XLA Ops:
  7.2 0.0 all-gather.6.cloned.1.call-start
  7.2 0.7 all-gather.6.cloned.1.call-update
  7.9 0.0 reduce-scatter.4.cloned.1.call-start
  7.9 38.8 %all-gather.6.cloned.1.call-done = bf16[512,4096]{1,0:T(8,128)(2,1)} async-done(((bf16[128,4096]{1,0:T(8,128)(2,1)}), bf16[512,4096]{1,0:T(8,128)(2,1)}) %all-gather.6.cloned.1.call-update) | async-done | bytes 4194320 | tf_op jit(solution)/shard_map/all_gather | solution.py:18
  46.7 23.9 %fusion.21 = f32[512,4096]{1,0:T(8,128)} fusion(bf16[512,4096]{1,0:T(8,128)(2,1)} %all-gather.6.cloned.1.call-done, bf16[4096,4096]{1,0:T(8,128)(2,1)} %param.9), kind=kOutput, calls=%fused_computation.38 | convolution fusion | flops 17179869184 | bytes 46137344 | tf_op jit(solution)/shard_map/dot_general | solution.py:21
  70.7 0.0 copy-start.2
  70.7 0.0 reduce-scatter.4.cloned.1.call-update
  70.7 1.2 copy-done.2
  71.9 1.1 copy.18
  72.9 5.5 all-to-all-start
  78.5 0.0 all-gather.8.cloned.1.call-start
  78.5 0.8 dynamic_slice.13
  79.3 52.0 %all-to-all-done = f32[64,8,512]{2,0,1:T(8,128)S(1)} async-done(((f32[64,8,512]{2,0,1:T(8,128)}), f32[64,8,512]{2,0,1:T(8,128)S(1)}, u32[]{:S(2)}, u32[]{:S(2)}) %all-to-all-start) | async-done | bytes 1048608 | tf_op jit(solution)/shard_map/all_to_all | solution.py:28
  131.2 0.4 fusion.20
  131.6 111.4 %reduce-scatter.4.cloned.1.call-done = f32[512,512]{1,0:T(8,128)} async-done(((f32[512,4096]{1,0:T(8,128)}), f32[512,512]{1,0:T(8,128)}) %reduce-scatter.4.cloned.1.call-update) | async-done | bytes 1048592 | tf_op jit(solution)/shard_map/reduce_scatter | solution.py:24
  243.1 2.7 divide_convert_fusion.1
  245.8 0.0 all-gather.8.cloned.1.call-update
  245.9 0.0 reduce-scatter.6.cloned.1.call-start
  245.9 73.8 %all-gather.8.cloned.1.call-done = bf16[512,4096]{1,0:T(8,128)(2,1)} async-done(((bf16[512,512]{1,0:T(8,128)(2,1)}), bf16[512,4096]{1,0:T(8,128)(2,1)}) %all-gather.8.cloned.1.call-update) | async-done | bytes 4194320 | tf_op jit(solution)/shard_map/all_gather | solution.py:31
  319.8 24.0 %fusion.22 = f32[512,4096]{1,0:T(8,128)} fusion(bf16[512,4096]{1,0:T(8,128)(2,1)} %all-gather.8.cloned.1.call-done, bf16[4096,4096]{1,0:T(8,128)(2,1)} %param.9), kind=kOutput, calls=%fused_computation.39 | convolution fusion | flops 17179869184 | bytes 46137344 | tf_op jit(solution)/shard_map/dot_general | solution.py:34
  343.8 0.0 copy-start.1
  343.8 0.0 reduce-scatter.6.cloned.1.call-update
  343.8 1.6 copy-done.1
  345.4 1.5 copy.17
  346.9 4.5 all-to-all-start.1
  351.3 0.0 all-gather.10.cloned.1.call-start
  351.4 0.0 dynamic-slice-start
  351.4 36.0 %all-to-all-done.1 = f32[128,4,1024]{2,0,1:T(8,128)} async-done(((f32[128,4,1024]{2,0,1:T(8,128)}), f32[128,4,1024]{2,0,1:T(8,128)}, u32[]{:S(2)}, u32[]{:S(2)}) %all-to-all-start.1) | async-done | bytes 2097184 | tf_op jit(solution)/shard_map/all_to_all | solution.py:44
  387.4 3.8 fusion.19
  391.2 32.3 %reduce-scatter.6.cloned.1.call-done = f32[512,1024]{1,0:T(8,128)} async-done(((f32[512,4096]{1,0:T(8,128)}), f32[512,1024]{1,0:T(8,128)}) %reduce-scatter.6.cloned.1.call-update) | async-done | bytes 2097168 | tf_op jit(solution)/shard_map/reduce_scatter | solution.py:42
  423.4 0.0 dynamic-slice-done
  423.4 3.9 fusion.11
  427.3 0.0 all-gather.10.cloned.1.call-update
  427.3 0.2 reduce-scatter.8.cloned.1.call-start
  427.5 31.7 %all-gather.10.cloned.1.call-done = bf16[512,4096]{1,0:T(8,128)(2,1)} async-done(((bf16[512,1024]{1,0:T(8,128)(2,1)}), bf16[512,4096]{1,0:T(8,128)(2,1)}) %all-gather.10.cloned.1.call-update) | async-done | bytes 4194320 | tf_op jit(solution)/shard_map/all_gather | solution.py:48
  459.3 23.9 %fusion.23 = f32[512,4096]{1,0:T(8,128)} fusion(bf16[512,4096]{1,0:T(8,128)(2,1)} %all-gather.10.cloned.1.call-done, bf16[4096,4096]{1,0:T(8,128)(2,1)} %param.9), kind=kOutput, calls=%fused_computation.40 | convolution fusion | flops 17179869184 | bytes 46137344 | tf_op jit(solution)/shard_map/dot_general | solution.py:21
  483.2 0.0 reduce-scatter.8.cloned.1.call-update
  483.2 0.0 all-gather.12.cloned.1.call-start
  483.3 0.7 all-gather.12.cloned.1.call-update
  484.0 0.0 all-gather.14.cloned.1.call-start
  484.0 147.2 %reduce-scatter.8.cloned.1.call-done = f32[512,512]{1,0:T(8,128)} async-done(((f32[512,4096]{1,0:T(8,128)}), f32[512,512]{1,0:T(8,128)}) %reduce-scatter.8.cloned.1.call-update) | async-done | bytes 1048592 | tf_op jit(solution)/shard_map/reduce_scatter | solution.py:24
  631.2 2.3 divide_convert_fusion
  633.5 0.0 all-gather.14.cloned.1.call-update
  633.5 1.9 constant_dynamic-slice_fusion.1
  635.4 4.9 subtract_reduce_fusion.1
  640.3 0.6 broadcast_multiply_fusion.1
  640.9 2.3 constant_dynamic-slice_fusion
  643.3 63.8 %all-gather.12.cloned.1.call-done = bf16[512,4096]{1,0:T(8,128)(2,1)} async-done(((bf16[512,512]{1,0:T(8,128)(2,1)}), bf16[512,4096]{1,0:T(8,128)(2,1)}) %all-gather.12.cloned.1.call-update) | async-done | bytes 4194320 | tf_op jit(solution)/shard_map/all_gather | solution.py:32
  707.0 75.5 %all-gather.14.cloned.1.call-done = bf16[512,4096]{1,0:T(8,128)(2,1)} async-done(((bf16[512,512]{1,0:T(8,128)(2,1)}), bf16[512,4096]{1,0:T(8,128)(2,1)}) %all-gather.14.cloned.1.call-update) | async-done | bytes 4194320 | tf_op jit(solution)/shard_map/all_gather | solution.py:50
  782.5 0.0 copy-start
  782.5 5.1 subtract_reduce_fusion
  787.6 0.6 broadcast_multiply_fusion
  788.2 0.0 copy-done
  788.2 2.8 neg.31
  791.0 43.4 %multiply_convert_fusion = bf16[4096,4096]{1,0:T(8,128)(2,1)} fusion(bf16[512,4096]{1,0:T(8,128)(2,1)} %all-gather.10.cloned.1.call-done, bf16[512,4096]{1,0:T(8,128)(2,1)} %all-gather.6.cloned.1.call-done, bf16[512,4096]{1,0:T(8,128)(2,1)} %neg.31, bf16[512,4096]{1,0:T(8,128)(2,1)} %all-gather.12.cloned.1.call-done), kind=kOutput, calls=%fused_computation | convolution fusion | flops 34426847232 | bytes 50331648 | tf_op jit(solution)/shard_map/dot_general | solution.py:54
Async XLA Ops:
  7.2 39.6 %all-gather.6.cloned.1.call-start = ((), (), s32[]{:S(2)}) async-start(), calls=%async_computation.5 | async-start | bytes 5242880 | tf_op jit(solution)/shard_map/all_gather | solution.py:18
  7.9 235.2 %reduce-scatter.4.cloned.1.call-start = ((), (), s32[]{:S(2)}) async-start(), calls=%async_computation.6 | async-start | bytes 9437184 | tf_op jit(solution)/shard_map/reduce_scatter | solution.py:24
  70.7 1.2 copy-start.2
  72.9 58.3 %all-to-all-start = ((f32[64,8,512]{2,0,1:T(8,128)}), f32[64,8,512]{2,0,1:T(8,128)S(1)}, u32[]{:S(2)}, u32[]{:S(2)}) async-start(f32[64,8,512]{2,0,1:T(8,128)} %bitcast.61), calls=%async_computation.1 | async-start | bytes 2097152 | tf_op jit(solution)/shard_map/all_to_all | solution.py:28
  78.5 241.3 %all-gather.8.cloned.1.call-start = ((), (), s32[]{:S(2)}) async-start(), calls=%async_computation.7 | async-start | bytes 4718592 | tf_op jit(solution)/shard_map/all_gather | solution.py:31
  245.9 177.6 %reduce-scatter.6.cloned.1.call-start = ((), (), s32[]{:S(2)}) async-start(), calls=%async_computation.8 | async-start | bytes 10485760 | tf_op jit(solution)/shard_map/reduce_scatter | solution.py:42
  343.8 1.6 copy-start.1
  346.9 40.5 %all-to-all-start.1 = ((f32[128,4,1024]{2,0,1:T(8,128)}), f32[128,4,1024]{2,0,1:T(8,128)}, u32[]{:S(2)}, u32[]{:S(2)}) async-start(f32[128,4,1024]{2,0,1:T(8,128)} %bitcast.60), calls=%async_computation.3 | async-start | bytes 4194304 | tf_op jit(solution)/shard_map/all_to_all | solution.py:44
  351.3 107.9 %all-gather.10.cloned.1.call-start = ((), (), s32[]{:S(2)}) async-start(), calls=%async_computation.9 | async-start | bytes 5242880 | tf_op jit(solution)/shard_map/all_gather | solution.py:48
  351.4 72.0 %dynamic-slice-start = ((f32[4096]{0:T(1024)}, s32[]{:T(128)}), f32[1024]{0:T(1024)S(1)}, s32[]{:S(2)}) async-start(f32[4096]{0:T(1024)} %param.10, s32[]{:T(128)} %select_n.14), calls=%async_computation.13 | async-start | bytes 8704 | tf_op jit(solution)/shard_map/dynamic_slice | solution.py:38
  427.3 203.9 %reduce-scatter.8.cloned.1.call-start = ((), (), s32[]{:S(2)}) async-start(), calls=%async_computation.11 | async-start | bytes 9437184 | tf_op jit(solution)/shard_map/reduce_scatter | solution.py:24
  483.2 223.8 %all-gather.12.cloned.1.call-start = ((), (), s32[]{:S(2)}) async-start(), calls=%async_computation.10 | async-start | bytes 4718592 | tf_op jit(solution)/shard_map/all_gather | solution.py:32
  484.0 298.5 %all-gather.14.cloned.1.call-start = ((), (), s32[]{:S(2)}) async-start(), calls=%async_computation.12 | async-start | bytes 4718592 | tf_op jit(solution)/shard_map/all_gather | solution.py:50
  782.5 5.7 copy-start
Sparse Core Ops, SparseCore 0:
  9.5 37.1 all-gather.5
  70.8 172.2 reduce-scatter.3
  246.0 73.7 all-gather.7
  343.9 79.4 reduce-scatter.5
  427.4 31.7 all-gather.9
  483.3 147.8 reduce-scatter.7
  633.2 73.7 all-gather.11
  709.6 72.8 all-gather.13
where the time goes:
time: 842 us; the launch traced here: 841 us
  waiting for transfers between devices  664 us (79%)
  matrix products  115 us (14%)
  other arithmetic  27.1 us (3%)
  between operations  14.2 us (2%)
  starting transfers between devices  10.5 us (1%)
  local copies, waits for them, and re-layouts  10.3 us (1%)
    reduce_scatter x2, waiting for transfers between devices, hidden_field(): lax.psum_scatter(partial_value, 'row', scatter_dimension=1, tiled=True)  259 us
    all_gather x1, waiting for transfers between devices, on_device(): negative_full = lax.all_gather(probs_back, 'row', axis=1, tiled=True)  75.5 us
    all_gather x1, waiting for transfers between devices, on_device(): lax.all_gather(sample_pos, 'row', axis=1, tiled=True)  73.8 us
    all_gather x1, waiting for transfers between devices, on_device(): lax.all_gather(probs_pos, 'row', axis=1, tiled=True)  63.8 us
    all_to_all x1, waiting for transfers between devices, on_device(): lax.all_to_all(hidden_uniform, 'row', split_axis=1, concat_axis=0, tiled=...  52 us
    dot_general x2, matrix products, hidden_field(): partial_value = jnp.dot(source, weights, preferred_element_type=jnp.float32)  47.8 us
    dot_general x1, matrix products, on_device(): lax.dot_general(left_side, right_side, contract_batch, preferred_element_...  43.4 us
    all_gather x1, waiting for transfers between devices, on_device(): visible_full = lax.all_gather(visible_data, 'col', axis=0, tiled=True)  38.8 us
  transfers between devices with their start and end apart: 10, of which 10 were waited for; matrix products, arithmetic and copies ran while one was open for 2% of the time, Pallas kernels for 0%

commit v1 on v0

v1 whole, which is shorter than its diff:
```python
import jax
import jax.numpy as jnp
from jax import lax
from jax.sharding import PartitionSpec as P


def relaxed(field, uniform):
    return jax.nn.sigmoid(2.0 * (field + jnp.log(uniform) - jnp.log1p(-uniform)))


def scatter_sum(partial_value, axis):
    narrow = partial_value.astype(jnp.bfloat16)
    return lax.psum_scatter(narrow, axis, scatter_dimension=0, tiled=True).astype(jnp.float32)


def gather(value, axis):
    return lax.all_gather(value, axis, axis=0, tiled=True)


def on_device(visible_data, hidden_uniform, visible_uniform, weights, visible_bias, hidden_bias):
    batch_total = visible_data.shape[0] * lax.axis_size("col")
    transposed = (((1,), (1,)), ((), ()))
    contract_batch = (((0,), (0,)), ((), ()))
    visible_full = gather(visible_data, "col")

    def hidden_field(source):
        partial_value = jnp.dot(source, weights, preferred_element_type=jnp.float32)
        return scatter_sum(partial_value, "row") + hidden_bias

    field_pos = hidden_field(visible_full)
    probs_pos = jax.nn.sigmoid(field_pos).astype(jnp.bfloat16)
    sample_own = relaxed(field_pos, hidden_uniform).astype(jnp.bfloat16)
    sample_full = gather(sample_own, "row")
    visible_partial = lax.dot_general(
        sample_full, weights, transposed, preferred_element_type=jnp.float32
    )
    field_neg = scatter_sum(visible_partial, "col") + visible_bias
    recon_own = relaxed(field_neg, visible_uniform).astype(jnp.bfloat16)
    recon_full = gather(recon_own, "col")
    probs_full = gather(probs_pos, "row")
    probs_back = jax.nn.sigmoid(hidden_field(recon_full)).astype(jnp.bfloat16)
    negative_full = gather(probs_back, "row")
    left_side = jnp.concatenate([visible_full, recon_full], axis=0)
    right_side = jnp.concatenate([probs_full, -negative_full], axis=0)
    difference = lax.dot_general(
        left_side, right_side, contract_batch, preferred_element_type=jnp.float32
    )
    grad_weights = (difference / batch_total).astype(jnp.bfloat16)
    grad_visible = jnp.mean(
        visible_full.astype(jnp.float32) - recon_full.astype(jnp.float32), axis=0
    )
    grad_hidden = jnp.mean(
        probs_full.astype(jnp.float32) - negative_full.astype(jnp.float32), axis=0
    )
    return (grad_weights, grad_visible, grad_hidden, sample_own, recon_own)


def solution(mesh):
    placed = (
        P("col", "row"),
        P("row", "col"),
        P("col", "row"),
        P("row", "col"),
        P("row"),
        P("col"),
    )
    return jax.shard_map(
        on_device,
        mesh=mesh,
        in_specs=placed,
        out_specs=(P("row", "col"), P("row"), P("col"), P("row", "col"), P("col", "row")),
        check_vma=False,
    )
```

time: 842 us -> 659 us (0.78)
  waiting for transfers between devices: 664 us -> 507 us
  local copies, waits for them, and re-layouts: 10.3 us -> 0.02 us
  starting transfers between devices: 10.5 us -> 0.5 us
    all_to_all x2 -> x0, waiting for transfers between devices: 87.9 us -> none  [the longest x1 52 us: on_device(): lax.all_to_all(hidden_uniform, 'row', split_axis=1, concat_axis=0, tiled=...]
    reduce_scatter x3, waiting for transfers between devices: 291 us -> 219 us  [scatter_sum(): lax.psum_scatter(narrow, axis, scatter_dimension=0, tiled=True)]
    all_to_all x2 -> x0, starting transfers between devices: 9.99 us -> none  [the longest x1 5.51 us: on_device(): lax.all_to_all(hidden_uniform, 'row', split_axis=1, concat_axis=0, tiled=...]
  transfers between devices with their start and end apart: 10 -> 8, of which waited for: 10 -> 8; matrix products, arithmetic and copies ran while one was open for 2% -> 1% of each run, Pallas kernels for 0% -> 0%
where the time goes in v1:
time: 659 us
  waiting for transfers between devices  507 us (77%)
  matrix products  114 us (17%)
  other arithmetic  22.6 us (3%)
  between operations  14.2 us (2%)
    all_gather x5, waiting for transfers between devices, gather(): return lax.all_gather(value, axis, axis=0, tiled=True)  287 us
    reduce_scatter x3, waiting for transfers between devices, scatter_sum(): lax.psum_scatter(narrow, axis, scatter_dimension=0, tiled=True)  219 us
    dot_general x2, matrix products, hidden_field(): partial_value = jnp.dot(source, weights, preferred_element_type=jnp.float32)  47.1 us
    dot_general x1, matrix products, on_device(): lax.dot_general(left_side, right_side, contract_batch, preferred_element_...  43.4 us
    dot_general x1, matrix products, on_device(): lax.dot_general(sample_full, weights, transposed, preferred_element_type=...  23.7 us
  transfers between devices with their start and end apart: 8, of which 8 were waited for; matrix products, arithmetic and copies ran while one was open for 1% of the time, Pallas kernels for 0%

profile of v1, /device:TPU:0, one launch (start us, length us, event | category | flops | bytes accessed | tf_op | source)
XLA Modules:
  0.0 658.9 jit_solution(7479944351545597440)
XLA Ops:
  7.2 0.0 all-gather.6.cloned.1.call-start
  7.2 0.7 all-gather.6.cloned.1.call-update
  7.9 0.0 reduce-scatter.4.cloned.1.call-start
  7.9 38.8 %all-gather.6.cloned.1.call-done = bf16[512,4096]{1,0:T(8,128)(2,1)} async-done(((bf16[128,4096]{1,0:T(8,128)(2,1)}), bf16[512,4096]{1,0:T(8,128)(2,1)}) %all-gather.6.cloned.1.call-update) | async-done | bytes 4194320 | tf_op jit(solution)/shard_map/all_gather | solution.py:17
  46.8 23.6 %convolution_convert_fusion.2 = bf16[512,4096]{1,0:T(8,128)(2,1)} fusion(bf16[512,4096]{1,0:T(8,128)(2,1)} %all-gather.6.cloned.1.call-done, bf16[4096,4096]{1,0:T(8,128)(2,1)} %param.9), kind=kOutput, calls=%fused_computation.11 | convolution fusion | flops 17181966336 | bytes 41943040 | tf_op jit(solution)/shard_map/dot_general | solution.py:27
  70.3 0.0 copy-start.2
  70.3 0.0 copy-start.3
  70.3 0.0 reduce-scatter.4.cloned.1.call-update
  70.3 0.0 all-gather.8.cloned.1.call-start
  70.4 88.4 %reduce-scatter.4.cloned.1.call-done = bf16[64,4096]{1,0:T(8,128)(2,1)} async-done(((bf16[512,4096]{1,0:T(8,128)(2,1)}), bf16[64,4096]{1,0:T(8,128)(2,1)}) %reduce-scatter.4.cloned.1.call-update) | async-done | bytes 524304 | tf_op jit(solution)/shard_map/reduce_scatter | solution.py:13
  158.8 0.0 copy-done.2
  158.8 0.0 copy-done.3
  158.8 2.9 divide_convert_fusion.2
  161.7 0.0 all-gather.8.cloned.1.call-update
  161.7 0.0 reduce-scatter.6.cloned.1.call-start
  161.8 72.5 %all-gather.8.cloned.1.call-done = bf16[512,4096]{1,0:T(8,128)(2,1)} async-done(((bf16[64,4096]{1,0:T(8,128)(2,1)}), bf16[512,4096]{1,0:T(8,128)(2,1)}) %all-gather.8.cloned.1.call-update) | async-done | bytes 4194320 | tf_op jit(solution)/shard_map/all_gather | solution.py:17
  234.3 23.7 %convolution_convert_fusion.1 = bf16[512,4096]{1,0:T(8,128)(2,1)} fusion(bf16[512,4096]{1,0:T(8,128)(2,1)} %all-gather.8.cloned.1.call-done, bf16[4096,4096]{1,0:T(8,128)(2,1)} %param.9), kind=kOutput, calls=%fused_computation.10 | convolution fusion | flops 17181966336 | bytes 41943040 | tf_op jit(solution)/shard_map/dot_general | solution.py:34
  258.0 0.0 copy-start.1
  258.0 0.0 copy-start.4
  258.0 0.0 reduce-scatter.6.cloned.1.call-update
  258.0 0.0 all-gather.10.cloned.1.call-start
  258.0 43.2 %reduce-scatter.6.cloned.1.call-done = bf16[128,4096]{1,0:T(8,128)(2,1)} async-done(((bf16[512,4096]{1,0:T(8,128)(2,1)}), bf16[128,4096]{1,0:T(8,128)(2,1)}) %reduce-scatter.6.cloned.1.call-update) | async-done | bytes 1048592 | tf_op jit(solution)/shard_map/reduce_scatter | solution.py:13
  301.3 0.0 copy-done.1
  301.3 0.0 copy-done.4
  301.3 3.7 divide_convert_fusion
  304.9 0.0 all-gather.10.cloned.1.call-update
  305.0 0.2 reduce-scatter.8.cloned.1.call-start
  305.2 34.4 %all-gather.10.cloned.1.call-done = bf16[512,4096]{1,0:T(8,128)(2,1)} async-done(((bf16[128,4096]{1,0:T(8,128)(2,1)}), bf16[512,4096]{1,0:T(8,128)(2,1)}) %all-gather.10.cloned.1.call-update) | async-done | bytes 4194320 | tf_op jit(solution)/shard_map/all_gather | solution.py:17
  339.6 23.6 %convolution_convert_fusion = bf16[512,4096]{1,0:T(8,128)(2,1)} fusion(bf16[512,4096]{1,0:T(8,128)(2,1)} %all-gather.10.cloned.1.call-done, bf16[4096,4096]{1,0:T(8,128)(2,1)} %param.9), kind=kOutput, calls=%fused_computation.9 | convolution fusion | flops 17181966336 | bytes 41943040 | tf_op jit(solution)/shard_map/dot_general | solution.py:27
  363.1 0.0 reduce-scatter.8.cloned.1.call-update
  363.2 0.0 all-gather.12.cloned.1.call-start
  363.2 0.7 all-gather.12.cloned.1.call-update
  363.9 0.0 all-gather.14.cloned.1.call-start
  364.0 87.7 %reduce-scatter.8.cloned.1.call-done = bf16[64,4096]{1,0:T(8,128)(2,1)} async-done(((bf16[512,4096]{1,0:T(8,128)(2,1)}), bf16[64,4096]{1,0:T(8,128)(2,1)}) %reduce-scatter.8.cloned.1.call-update) | async-done | bytes 524304 | tf_op jit(solution)/shard_map/reduce_scatter | solution.py:13
  451.6 2.1 divide_convert_fusion.1
  453.7 0.0 all-gather.14.cloned.1.call-update
  453.7 4.9 subtract_reduce_fusion.1
  458.7 0.6 broadcast_multiply_fusion.1
  459.3 66.9 %all-gather.12.cloned.1.call-done = bf16[512,4096]{1,0:T(8,128)(2,1)} async-done(((bf16[64,4096]{1,0:T(8,128)(2,1)}), bf16[512,4096]{1,0:T(8,128)(2,1)}) %all-gather.12.cloned.1.call-update) | async-done | bytes 4194320 | tf_op jit(solution)/shard_map/all_gather | solution.py:17
  526.2 74.1 %all-gather.14.cloned.1.call-done = bf16[512,4096]{1,0:T(8,128)(2,1)} async-done(((bf16[64,4096]{1,0:T(8,128)(2,1)}), bf16[512,4096]{1,0:T(8,128)(2,1)}) %all-gather.14.cloned.1.call-update) | async-done | bytes 4194320 | tf_op jit(solution)/shard_map/all_gather | solution.py:17
  600.2 0.0 copy-start
  600.2 5.1 subtract_reduce_fusion
  605.3 0.6 broadcast_multiply_fusion
  605.9 0.0 copy-done
  605.9 2.8 neg.27
  608.7 43.4 %multiply_convert_fusion = bf16[4096,4096]{1,0:T(8,128)(2,1)} fusion(bf16[512,4096]{1,0:T(8,128)(2,1)} %all-gather.10.cloned.1.call-done, bf16[512,4096]{1,0:T(8,128)(2,1)} %all-gather.6.cloned.1.call-done, bf16[512,4096]{1,0:T(8,128)(2,1)} %neg.27, bf16[512,4096]{1,0:T(8,128)(2,1)} %all-gather.12.cloned.1.call-done), kind=kOutput, calls=%fused_computation | convolution fusion | flops 34426847232 | bytes 50331648 | tf_op jit(solution)/shard_map/dot_general | solution.py:45
Async XLA Ops:
  7.2 39.6 %all-gather.6.cloned.1.call-start = ((), (), s32[]{:S(2)}) async-start(), calls=%async_computation.3 | async-start | bytes 5242880 | tf_op jit(solution)/shard_map/all_gather | solution.py:17
  7.9 150.9 %reduce-scatter.4.cloned.1.call-start = ((), (), s32[]{:S(2)}) async-start(), calls=%async_computation.4 | async-start | bytes 4718592 | tf_op jit(solution)/shard_map/reduce_scatter | solution.py:13
  70.3 88.5 %copy-start.2 = (f32[64,4096]{1,0:T(8,128)S(1)}, f32[64,4096]{1,0:T(8,128)}, u32[]{:S(2)}) copy-start(f32[64,4096]{1,0:T(8,128)} %param.7) | copy-start | bytes 3145732
  70.3 88.5 %copy-start.3 = (f32[4096]{0:T(1024)S(1)}, f32[4096]{0:T(1024)}, u32[]{:S(2)}) copy-start(f32[4096]{0:T(1024)} %param.11) | copy-start | bytes 49156
  70.3 163.9 %all-gather.8.cloned.1.call-start = ((), (), s32[]{:S(2)}) async-start(), calls=%async_computation.5 | async-start | bytes 4718592 | tf_op jit(solution)/shard_map/all_gather | solution.py:17
  161.7 139.5 %reduce-scatter.6.cloned.1.call-start = ((), (), s32[]{:S(2)}) async-start(), calls=%async_computation.6 | async-start | bytes 5242880 | tf_op jit(solution)/shard_map/reduce_scatter | solution.py:13
  258.0 43.3 %copy-start.1 = (f32[128,4096]{1,0:T(8,128)S(1)}, f32[128,4096]{1,0:T(8,128)}, u32[]{:S(2)}) copy-start(f32[128,4096]{1,0:T(8,128)} %param.8) | copy-start | bytes 6291460
  258.0 43.3 %copy-start.4 = (f32[4096]{0:T(1024)S(1)}, f32[4096]{0:T(1024)}, u32[]{:S(2)}) copy-start(f32[4096]{0:T(1024)} %param.10) | copy-start | bytes 49156
  258.0 81.6 %all-gather.10.cloned.1.call-start = ((), (), s32[]{:S(2)}) async-start(), calls=%async_computation.7 | async-start | bytes 5242880 | tf_op jit(solution)/shard_map/all_gather | solution.py:17
  305.0 146.7 %reduce-scatter.8.cloned.1.call-start = ((), (), s32[]{:S(2)}) async-start(), calls=%async_computation.9 | async-start | bytes 4718592 | tf_op jit(solution)/shard_map/reduce_scatter | solution.py:13
  363.2 163.0 %all-gather.12.cloned.1.call-start = ((), (), s32[]{:S(2)}) async-start(), calls=%async_computation.8 | async-start | bytes 4718592 | tf_op jit(solution)/shard_map/all_gather | solution.py:17
  363.9 236.3 %all-gather.14.cloned.1.call-start = ((), (), s32[]{:S(2)}) async-start(), calls=%async_computation.10 | async-start | bytes 4718592 | tf_op jit(solution)/shard_map/all_gather | solution.py:17
  600.2 5.7 copy-start
Sparse Core Ops, SparseCore 0:
  9.5 37.1 all-gather.5
  70.5 88.2 reduce-scatter.3
  161.8 72.3 all-gather.7
  258.1 43.1 reduce-scatter.5
  305.1 34.4 all-gather.9
  363.3 88.2 reduce-scatter.7
  453.7 72.3 all-gather.11
  528.9 71.3 all-gather.13
